TPU v7x, 32 devices: a whole 2x2x4 slice. The times are simulated.
32 devices in a mesh: seq: 8 (over z, y), mp: 4 (over x, core).
Axes of the slice: x: 2, y: 2, z: 4, core: 2. Of those that a mesh axis runs over, the one named last changes fastest.
Arguments:
- hidden_in: bfloat16 [2, 1024, 2048], P(None, 'seq'), may hold values from -6 to 6
- attn_gain: float32 [2048], replicated, may hold values from 0.1 to 1.9
- q_weight: bfloat16 [2048, 2048], P(None, 'mp'), may hold values from -0.125 to 0.125
- q_bias: float32 [2048], P('mp'), may hold values from -60 to 60
- k_weight: bfloat16 [2048, 256], replicated, may hold values from -0.125 to 0.125
- k_bias: float32 [256], replicated, may hold values from -60 to 60
- v_weight: bfloat16 [2048, 256], replicated, may hold values from -0.125 to 0.125
- v_bias: float32 [256], replicated, may hold values from -3 to 3
- o_weight: bfloat16 [2048, 2048], P('mp'), may hold values from -0.125 to 0.125
- mlp_gain: float32 [2048], replicated, may hold values from 0.1 to 1.9
- gate_weight: bfloat16 [2048, 5632], P('seq', 'mp'), may hold values from -0.125 to 0.125
- up_weight: bfloat16 [2048, 5632], P('seq', 'mp'), may hold values from -0.125 to 0.125
- down_weight: bfloat16 [2048, 5632], P('seq', 'mp'), may hold values from -0.078125 to 0.078125
- lengths: int32 [2], replicated, may hold values from 512 to 1024
Outputs:
- layer_out: bfloat16 [2, 1024, 2048], P(None, 'seq', 'mp')
- influence: float32 [2, 1024], P(None, 'seq')
- score: float32 [2], replicated
Inputs may be any that keep to these rules, and one draw needn't show every extreme that they name: `lengths`: tokens at positions 512 and later may be invalid.
All inputs are finite; a program needn't handle non-finite values.
Results may differ from a plain program's by a relative error of at most 0.02.
The roundings to bfloat16 on the way count: a program that leaves them out, or rounds other values in their place, can miss the bound.
Values may be sent and summed in bfloat16 or wider, within the bound.
A program may use at most 192 MiB of HBM per device.

v0:
```python
import jax
import jax.numpy as jnp
from jax import lax
from jax.sharding import PartitionSpec as P

HEADS = 16
KV_HEADS = 2
HEAD = 128


rope_base = 1000000.0
norm_eps = 1e-06
masked_score = -1e30


def rms_scale(values, gain):
    widened = values.astype(jnp.float32)
    factor = lax.rsqrt(jnp.mean(widened * widened, axis=-1, keepdims=True) + norm_eps)
    return (widened * factor * gain).astype(jnp.bfloat16)


def rotate(values, positions):
    head_width = values.shape[-1]
    half_width = head_width // 2
    inv_freq = rope_base ** (-(jnp.arange(half_width, dtype=jnp.float32) * 2.0) / head_width)
    angles = positions.astype(jnp.float32)[:, None] * inv_freq[None, :]
    angles = jnp.concatenate([angles, angles], axis=-1)
    first_part = values[..., :half_width]
    second_part = values[..., half_width:]
    turned = jnp.concatenate([-second_part, first_part], axis=-1)
    return values * jnp.cos(angles) + turned * jnp.sin(angles)


def attend_update(state, queries, first_pos, key_piece, value_piece):
    run_max, run_sum, run_acc = state
    score_scale = queries.shape[-1] ** (-0.5)
    query_pos = first_pos + jnp.arange(queries.shape[2], dtype=jnp.int32)
    key_pos = jnp.arange(key_piece.shape[1], dtype=jnp.int32)
    scores = (
        jnp.einsum("shqd,skd->shqk", queries, key_piece, preferred_element_type=jnp.float32)
        * score_scale
    )
    allowed = key_pos[None, :] <= query_pos[:, None]
    scores = jnp.where(allowed, scores, masked_score)
    new_max = jnp.maximum(run_max, jnp.max(scores, axis=-1))
    weights = jnp.where(allowed, jnp.exp(scores - new_max[..., None]), 0.0)
    new_sum = jnp.sum(weights, axis=-1)
    mixed = jnp.einsum(
        "shqk,skd->shqd",
        weights.astype(jnp.bfloat16),
        value_piece,
        preferred_element_type=jnp.float32,
    )
    return (new_max, new_sum, mixed)


def local(
    hidden_in,
    attn_gain,
    q_weight,
    q_bias,
    k_weight,
    k_bias,
    v_weight,
    v_bias,
    o_weight,
    mlp_gain,
    gate_weight,
    up_weight,
    down_weight,
    lengths,
):
    seqs_n, tok_n, width = hidden_in.shape
    seq_rank = lax.axis_index("seq")
    mp_devices = lax.axis_size("mp")
    mp_rank = lax.axis_index("mp")
    heads_here = q_weight.shape[1] // HEAD
    group_size = HEADS // KV_HEADS
    kv_index = mp_rank * heads_here // group_size
    flat_in = hidden_in.reshape(seqs_n * tok_n, width)
    normed = rms_scale(flat_in, attn_gain)
    query_all = jnp.dot(normed, q_weight, preferred_element_type=jnp.float32) + q_bias
    key_cols = lax.dynamic_slice_in_dim(k_weight, kv_index * HEAD, HEAD, 1)
    value_cols = lax.dynamic_slice_in_dim(v_weight, kv_index * HEAD, HEAD, 1)
    key_shift = lax.dynamic_slice_in_dim(k_bias, kv_index * HEAD, HEAD, 0)
    value_shift = lax.dynamic_slice_in_dim(v_bias, kv_index * HEAD, HEAD, 0)
    key_all = jnp.dot(normed, key_cols, preferred_element_type=jnp.float32) + key_shift
    value_rows = (
        jnp.dot(normed, value_cols, preferred_element_type=jnp.float32) + value_shift
    ).astype(jnp.bfloat16)
    positions = seq_rank * tok_n + jnp.arange(tok_n, dtype=jnp.int32)
    rotated_q = rotate(
        query_all.reshape(seqs_n, tok_n, heads_here, HEAD).transpose(0, 2, 1, 3), positions
    ).astype(jnp.bfloat16)
    rotated_k = rotate(key_all.reshape(seqs_n, tok_n, HEAD), positions).astype(jnp.bfloat16)
    value_rows = value_rows.reshape(seqs_n, tok_n, HEAD)
    query_sets = ((rotated_q, seq_rank * tok_n),)
    initial = tuple(
        (
            (
                jnp.full(entry[0].shape[:3], masked_score, jnp.float32),
                jnp.zeros(entry[0].shape[:3], jnp.float32),
                jnp.zeros(entry[0].shape, jnp.float32),
            )
            for entry in query_sets
        )
    )
    key_start = jnp.int32(0)
    key_piece = lax.all_gather(rotated_k, "seq", axis=1, tiled=True)
    value_piece = lax.all_gather(value_rows, "seq", axis=1, tiled=True)
    updated = []
    for state, query_entry in zip(initial, query_sets):
        queries, first_pos = query_entry
        last_pos = first_pos + queries.shape[2] - 1

        def run_update(current):
            return attend_update(current, queries, first_pos, key_piece, value_piece)

        def keep_state(current):
            return current

        updated.append(lax.cond(key_start <= last_pos, run_update, keep_state, state))
    results = tuple(updated)
    finished = [(entry[2] / entry[1][..., None]).astype(jnp.bfloat16) for entry in results]
    attn = finished[0]
    attn = attn.transpose(0, 2, 1, 3).reshape(seqs_n * tok_n, heads_here * HEAD)
    projected = jnp.dot(attn, o_weight, preferred_element_type=jnp.float32)
    quarter = width // mp_devices
    own_in = lax.dynamic_slice_in_dim(flat_in, mp_rank * quarter, quarter, 1)
    summed = lax.psum(projected.astype(jnp.bfloat16), "mp").astype(jnp.float32)
    residual = (flat_in.astype(jnp.float32) + summed).astype(jnp.bfloat16)
    resid_part = lax.dynamic_slice_in_dim(residual, mp_rank * quarter, quarter, 1)
    mlp_in = rms_scale(residual, mlp_gain)
    gate_sum = jnp.dot(
        mlp_in,
        lax.all_gather(gate_weight, "seq", axis=0, tiled=True),
        preferred_element_type=jnp.float32,
    )
    up_sum = jnp.dot(
        mlp_in,
        lax.all_gather(up_weight, "seq", axis=0, tiled=True),
        preferred_element_type=jnp.float32,
    )
    activated = (jax.nn.silu(gate_sum) * up_sum).astype(jnp.bfloat16)
    down_part = lax.dot_general(
        activated,
        lax.all_gather(down_weight, "seq", axis=0, tiled=True),
        (((1,), (1,)), ((), ())),
        preferred_element_type=jnp.float32,
    )
    mlp_share = lax.psum_scatter(
        down_part.astype(jnp.bfloat16), "mp", scatter_dimension=1, tiled=True
    ).astype(jnp.float32)
    layer_part = (resid_part.astype(jnp.float32) + mlp_share).astype(jnp.bfloat16)
    in_share = own_in.astype(jnp.float32)
    out_share = layer_part.astype(jnp.float32)
    cross_part = jnp.sum(in_share * out_share, axis=-1).reshape(seqs_n, tok_n)
    out_part = jnp.sum(out_share * out_share, axis=-1).reshape(seqs_n, tok_n)
    cross, out_norm = lax.psum((cross_part, out_part), "mp")
    in_wide = flat_in.astype(jnp.float32)
    in_norm = jnp.sum(in_wide * in_wide, axis=-1).reshape(seqs_n, tok_n)
    cosine = cross / jnp.sqrt((in_norm + norm_eps) * (out_norm + norm_eps))
    valid = positions[None, :] < lengths[:, None]
    influence = jnp.where(valid, 1.0 - cosine, 0.0)
    seq_total = lax.psum(jnp.sum(influence, axis=1), "seq")
    score = seq_total / lengths.astype(jnp.float32)
    return (layer_part.reshape(seqs_n, tok_n, quarter), influence, score)


def solution(mesh):
    placed = (
        P(None, "seq", None),
        P(),
        P(None, "mp"),
        P("mp"),
        P(),
        P(),
        P(),
        P(),
        P("mp", None),
        P(),
        P("seq", "mp"),
        P("seq", "mp"),
        P("seq", "mp"),
        P(),
    )
    return jax.shard_map(
        local,
        mesh=mesh,
        in_specs=placed,
        out_specs=(P(None, "seq", "mp"), P(None, "seq"), P()),
        check_vma=False,
    )
```

profile of v0, /device:TPU:0, one launch (start us, length us, event | category | flops | bytes accessed | tf_op | source)
XLA Modules:
  0.0 447.5 jit_solution(1680391220494171423)
XLA Ops:
  8.1 1.6 multiply_reduce_fusion
  10.6 1.5 fusion.14
  13.8 1.2 fusion.34
  15.0 35.3 %all_gather.15 = bf16[2,1024,128]{2,1,0:T(8,128)(2,1)} all-gather(bf16[2,128,128]{2,1,0:T(8,128)(2,1)S(1)} %fusion.34), channel_id=1, replica_groups=mesh['seq'=8,'mp'=4] {'seq'}, dimensions={1}, use_global_device_ids=true | all-gather | bytes 589824 | tf_op jit(solution)/shard_map/all_gather | solution.py:109
  50.3 1.5 fusion.19
  51.8 33.2 %all_gather.16 = bf16[2,1024,128]{2,1,0:T(8,128)(2,1)} all-gather(bf16[2,128,128]{2,1,0:T(8,128)(2,1)S(1)} %bitcast.49), channel_id=1, replica_groups=mesh['seq'=8,'mp'=4] {'seq'}, dimensions={1}, use_global_device_ids=true | all-gather | bytes 589824 | tf_op jit(solution)/shard_map/all_gather | solution.py:110
  85.0 1.5 convolution_add_fusion
  86.5 1.2 reshape.194
  87.8 1.2 slice_negate_fusion
  88.9 1.4 fusion.23
  90.4 3.7 conditional.1
  92.7 1.3 fusion.2
  94.5 1.7 convolution_convert_fusion
  98.2 35.9 %all-reduce.3.cloned.1.call-done = bf16[256,2048]{1,0:T(8,128)(2,1)} async-done(((bf16[256,2048]{1,0:T(8,128)(2,1)}), bf16[256,2048]{1,0:T(8,128)(2,1)}) %all-reduce.3.cloned.1.call-update) | async-done | bytes 1048592 | tf_op jit(solution)/shard_map/psum | solution.py:130
  134.1 2.6 fusion.16
  136.7 55.5 %all-gather.4.cloned.1.call-done = bf16[2048,1408]{1,0:T(8,128)(2,1)} async-done(((bf16[256,1408]{1,0:T(8,128)(2,1)}), bf16[2048,1408]{1,0:T(8,128)(2,1)}) %all-gather.4.cloned.1.call-update) | async-done | bytes 5767184 | tf_op jit(solution)/shard_map/all_gather | solution.py:136
  192.2 6.0 %fusion.28 = f32[256,1408]{1,0:T(8,128)} fusion(bf16[2048,1408]{1,0:T(8,128)(2,1)} %all-gather.4.cloned.1.call-done, bf16[256,2048]{1,0:T(8,128)(2,1)} %get-tuple-element.27, f32[2048]{0:T(1024)S(1)} %copy-done.7, f32[256]{0:T(256)S(1)} %add_rsqrt_fusion), kind=kOutput, calls=%fused_computation.48 | convolution fusion | flops 1478492160 | bytes 8266752 | tf_op jit(solution)/shard_map/dot_general | solution.py:134
  198.2 86.4 %all-gather.6.cloned.1.call-done = bf16[2048,1408]{1,0:T(8,128)(2,1)} async-done(((bf16[256,1408]{1,0:T(8,128)(2,1)}), bf16[2048,1408]{1,0:T(8,128)(2,1)}) %all-gather.6.cloned.1.call-update) | async-done | bytes 5767184 | tf_op jit(solution)/shard_map/all_gather | solution.py:141
  284.6 92.4 %all-gather.8.cloned.1.call-done = bf16[2048,1408]{1,0:T(8,128)(2,1)} async-done(((bf16[256,1408]{1,0:T(8,128)(2,1)}), bf16[2048,1408]{1,0:T(8,128)(2,1)}) %all-gather.8.cloned.1.call-update) | async-done | bytes 5767184 | tf_op jit(solution)/shard_map/all_gather | solution.py:147
  376.9 9.5 %convolution_convert_fusion.1 = bf16[256,2048]{1,0:T(8,128)(2,1)} fusion(bf16[2048,1408]{1,0:T(8,128)(2,1)} %all-gather.8.cloned.1.call-done, bf16[2048,1408]{1,0:T(8,128)(2,1)} %all-gather.6.cloned.1.call-done, f32[256,1408]{1,0:T(8,128)} %fusion.28, bf16[256,2048]{1,0:T(8,128)(2,1)} %get-tuple-element.27, f32[2048]{0:T(1024)S(1)} %copy-done.7, ...), kind=kOutput, calls=%fused_computation.23 | convolution fusion | flops 2957574144 | bytes 15082496 | tf_op jit(solution)/shard_map/dot_general | solution.py:145
  386.5 23.1 %reduce-scatter.2.cloned.1.call-done = bf16[256,512]{1,0:T(8,128)(2,1)} async-done(((bf16[256,2048]{1,0:T(8,128)(2,1)}), bf16[256,512]{1,0:T(8,128)(2,1)}) %reduce-scatter.2.cloned.1.call-update) | async-done | bytes 262160 | tf_op jit(solution)/shard_map/reduce_scatter | solution.py:151
  409.5 1.8 fusion.21
  411.4 5.7 %all-reduce = (f32[2,128]{1,0:T(2,128)S(1)}, f32[2,128]{1,0:T(2,128)S(1)}) all-reduce(f32[2,128]{1,0:T(2,128)S(1)} %bitcast.52, f32[2,128]{1,0:T(2,128)S(1)} %bitcast.51), channel_id=1, replica_groups=mesh['seq'=8,'mp'=4] {'mp'}, use_global_device_ids=true, to_apply=%region_9.10 | all-reduce | flops 512 | bytes 4096 | tf_op jit(solution)/shard_map/psum | solution.py:159
  417.8 21.5 %psum.31 = f32[2]{0:T(128)S(1)} all-reduce(f32[2]{0:T(128)S(1)} %get-tuple-element.23), channel_id=1, replica_groups=mesh['seq'=8,'mp'=4] {'seq'}, use_global_device_ids=true, to_apply=%region_13.14 | all-reduce | flops 2 | bytes 16 | tf_op jit(solution)/shard_map/psum | solution.py:165
  (51 shorter events, 8.5 us)
Async XLA Ops:
  8.0 86.5 %copy-start = (bf16[512,2048]{1,0:T(8,128)(2,1)S(1)}, bf16[512,2048]{1,0:T(8,128)(2,1)}, u32[]{:S(2)}) copy-start(bf16[512,2048]{1,0:T(8,128)(2,1)} %param.24) | copy-start | bytes 6291460
  8.0 126.1 %all-reduce.3.cloned.1.call-start = ((), (), s32[]{:S(2)}) async-start(), calls=%async_computation.1 | async-start | bytes 2097152 | tf_op jit(solution)/shard_map/psum | solution.py:130
  9.8 2.4 copy-start.4
  12.2 38.1 %copy-start.9 = (f32[256]{0:T(256)S(1)}, f32[256]{0:T(256)}, u32[]{:S(2)}) copy-start(f32[256]{0:T(256)} %param.23) | copy-start | bytes 3076
  12.6 72.4 %copy-start.8 = (f32[512]{0:T(512)S(1)}, f32[512]{0:T(512)}, u32[]{:S(2)}) copy-start(f32[512]{0:T(512)} %param.19) | copy-start | bytes 6148
  13.3 71.7 %copy-start.6 = (bf16[2048,512]{1,0:T(8,128)(2,1)S(1)}, bf16[2048,512]{1,0:T(8,128)(2,1)}, u32[]{:S(2)}) copy-start(bf16[2048,512]{1,0:T(8,128)(2,1)} %param.18) | copy-start | bytes 6291460
  87.8 2.6 copy-start.2
  90.5 1.0 copy-start.3
  96.2 38.0 %copy-start.1 = (bf16[2,128,2048]{2,1,0:T(8,128)(2,1)S(1)}, bf16[2,128,2048]{2,1,0:T(8,128)(2,1)}, u32[]{:S(2)}) copy-start(bf16[2,128,2048]{2,1,0:T(8,128)(2,1)} %param.16) | copy-start | bytes 3145732
  96.2 96.0 %all-gather.4.cloned.1.call-start = ((), (), s32[]{:S(2)}) async-start(), calls=%async_computation.2 | async-start | bytes 6488064 | tf_op jit(solution)/shard_map/all_gather | solution.py:136
  96.8 187.8 %all-gather.6.cloned.1.call-start = ((), (), s32[]{:S(2)}) async-start(), calls=%async_computation.3 | async-start | bytes 6488064 | tf_op jit(solution)/shard_map/all_gather | solution.py:141
  97.4 94.9 %copy-start.7 = (f32[2048]{0:T(1024)S(1)}, f32[2048]{0:T(1024)}, u32[]{:S(2)}) copy-start(f32[2048]{0:T(1024)} %param.25) | copy-start | bytes 24580
  97.4 279.5 %all-gather.8.cloned.1.call-start = ((), (), s32[]{:S(2)}) async-start(), calls=%async_computation.4 | async-start | bytes 6488064 | tf_op jit(solution)/shard_map/all_gather | solution.py:147
  97.9 311.6 %reduce-scatter.2.cloned.1.call-start = ((), (), s32[]{:S(2)}) async-start(), calls=%async_computation.5 | async-start | bytes 1310720 | tf_op jit(solution)/shard_map/reduce_scatter | solution.py:151
  386.4 30.7 %copy-start.5 = (s32[2]{0:T(128)S(1)}, s32[2]{0:T(128)}, u32[]{:S(2)}) copy-start(s32[2]{0:T(128)} %param.29) | copy-start | bytes 28
Sparse Core Ops, SparseCore 0:
  96.3 37.7 all-reduce.2
  386.6 22.9 reduce-scatter.1
Sparse Core Ops, SparseCore 1:
  98.9 93.3 all-gather.3
  194.3 90.2 all-gather.5
  286.6 90.2 all-gather.7
where the time goes:
time: 448 us; the launch traced here: 447 us
  waiting for transfers between devices  295 us (66%)
  blocking collectives  95.7 us (21%)
  matrix products  22.6 us (5%)
  between operations  15.9 us (4%)
  other arithmetic  15.5 us (3%)
    all_gather x1, waiting for transfers between devices, local(): lax.all_gather(down_weight, 'seq', axis=0, tiled=True)  92.4 us
    all_gather x1, waiting for transfers between devices, local(): lax.all_gather(up_weight, 'seq', axis=0, tiled=True)  86.4 us
    all_gather x1, waiting for transfers between devices, local(): lax.all_gather(gate_weight, 'seq', axis=0, tiled=True)  55.5 us
    psum x1, waiting for transfers between devices, local(): summed = lax.psum(projected.astype(jnp.bfloat16), 'mp').astype(jnp.float32)  35.9 us
    all_gather x1, blocking collectives, local(): key_piece = lax.all_gather(rotated_k, 'seq', axis=1, tiled=True)  35.3 us
    all_gather x1, blocking collectives, local(): value_piece = lax.all_gather(value_rows, 'seq', axis=1, tiled=True)  33.2 us
    reduce_scatter x1, waiting for transfers between devices, local(): lax.psum_scatter(down_part.astype(jnp.bfloat16), 'mp', scatter_dimension=...  23.1 us
    psum x1, blocking collectives, local(): seq_total = lax.psum(jnp.sum(influence, axis=1), 'seq')  21.5 us
  transfers between devices with their start and end apart: 5, of which 5 were waited for; matrix products, arithmetic and copies ran while one was open for 2% of the time, Pallas kernels for 0%

commit v1 on v0

--- a/solution.py
+++ b/solution.py
@@ -1,6 +1,10 @@
+import functools
+
 import jax
 import jax.numpy as jnp
 from jax import lax
+from jax.experimental import pallas as pl
+from jax.experimental.pallas import tpu as pltpu
 from jax.sharding import PartitionSpec as P
 
 HEADS = 16
@@ -167,6 +171,490 @@
     return (layer_part.reshape(seqs_n, tok_n, quarter), influence, score)
 
 
+MESH = pl.DeviceIdType.MESH
+PAIR = 2
+VMEM_BYTES = 60 * 1024 * 1024
+
+
+def layer_kernel(
+    n,
+    m,
+    q_ref,
+    kv_ref,
+    w_ref,
+    o_ref,
+    h_ref,
+    g_ref,
+    out_ref,
+    kv_all,
+    w_all,
+    attn,
+    part,
+    rs_buf,
+    resid,
+    mlp_in,
+    sums,
+    c_buf,
+    b_buf,
+    a_buf,
+    z_buf,
+    kv_send,
+    kv_recv,
+    fw_send,
+    fw_recv,
+    w_send,
+    w_recv,
+    rs_send,
+    rs_recv,
+    zg_send,
+    ag_send,
+    ag_recv,
+    c_send,
+    c_recv,
+    b_send,
+    b_recv,
+    a_send,
+    a_recv,
+    zs_send,
+    zs_recv,
+):
+    f32, bf16 = jnp.float32, jnp.bfloat16
+    s = lax.axis_index("seq")
+    mp = lax.axis_index("mp")
+    nz = n // PAIR
+    nx = m // PAIR
+    z, y = s // PAIR, s % PAIR
+    x, c = mp // PAIR, mp % PAIR
+    tok, width_q = h_ref.shape
+    seqs_n, heads_here, tok_n, head_w = q_ref.shape
+    rows = w_ref.shape[3]
+
+    def seq_of(zz, yy):
+        return zz * PAIR + yy
+
+    def mp_of(xx, cc):
+        return xx * PAIR + cc
+
+    ya, xa = y + (1 - c) * (1 - 2 * y), x + c * (1 - 2 * x)
+    yb, xb = y + c * (1 - 2 * y), x + (1 - c) * (1 - 2 * x)
+    dev_a = (seq_of(z, ya), mp_of(xa, c))
+    dev_b = (seq_of(z, yb), mp_of(xb, c))
+    dev_c = (s, mp_of(x, 1 - c))
+
+    def remote(source, target, sent, arrived, device):
+        return pltpu.make_async_remote_copy(
+            src_ref=source,
+            dst_ref=target,
+            send_sem=sent,
+            recv_sem=arrived,
+            device_id=device,
+            device_id_type=MESH,
+        )
+
+    barrier = pltpu.get_barrier_semaphore()
+    for d in range(1, n):
+        pl.semaphore_signal(barrier, inc=1, device_id=((s + d) % n, mp), device_id_type=MESH)
+    for d in range(1, m):
+        pl.semaphore_signal(barrier, inc=1, device_id=(s, (mp + d) % m), device_id_type=MESH)
+    pl.semaphore_wait(barrier, n - 1 + m - 1)
+
+    def kv_copy(d):
+        return remote(
+            kv_ref.at[c], kv_all.at[c, s], kv_send.at[d], kv_recv.at[s], ((s + d) % n, mp)
+        )
+
+    def w_copy(d):
+        peer = (s + d) % n
+        here = pl.ds(pl.multiple_of(s * rows, rows), rows)
+        return remote(
+            w_ref.at[:, peer], w_all.at[:, :, here], w_send.at[d], w_recv.at[s], (peer, mp)
+        )
+
+    for d in range(1, n):
+        @pl.when((s + d) % n > s)
+        def _():
+            kv_copy(d).start()
+
+    for d in range(1, n):
+        w_copy(d).start()
+
+    kv_all[0, s] = kv_ref[0]
+    kv_all[1, s] = kv_ref[1]
+    w_all[:, :, pl.ds(pl.multiple_of(s * rows, rows), rows)] = w_ref[:, s]
+    for j in range(n):
+        @pl.when(j > s)
+        def _():
+            kv_all[0, j] = jnp.zeros_like(kv_ref[0])
+            kv_all[1, j] = jnp.zeros_like(kv_ref[1])
+
+    def fw_copy(j, cc):
+        return remote(kv_all.at[cc, j], kv_all.at[cc, j], fw_send.at[j], fw_recv.at[j], dev_c)
+
+    for j in range(n):
+        @pl.when(j < s)
+        def _():
+            remote(kv_ref.at[c], kv_all.at[c, j], kv_send.at[0], kv_recv.at[j], dev_c).wait_recv()
+            fw_copy(j, c).start()
+
+    for j in range(n):
+        @pl.when(j < s)
+        def _():
+            fw_copy(j, 1 - c).wait_recv()
+
+    scale = head_w ** (-0.5)
+    query_pos = s * tok_n + lax.broadcasted_iota(jnp.int32, (tok_n, n * tok_n), 0)
+    key_pos = lax.broadcasted_iota(jnp.int32, (tok_n, n * tok_n), 1)
+    allowed = key_pos <= query_pos
+    for i in range(seqs_n):
+        keys = kv_all[0, :, i].reshape(n * tok_n, head_w)
+        vals = kv_all[1, :, i].reshape(n * tok_n, head_w)
+        for h in range(heads_here):
+            scores = lax.dot_general(
+                q_ref[i, h], keys, (((1,), (1,)), ((), ())), preferred_element_type=f32
+            )
+            scores = jnp.where(allowed, scores * scale, masked_score)
+            top = jnp.max(scores, axis=-1, keepdims=True)
+            weights = jnp.where(allowed, jnp.exp(scores - top), 0.0)
+            total = jnp.sum(weights, axis=-1, keepdims=True)
+            mixed = jnp.dot(weights.astype(bf16), vals, preferred_element_type=f32)
+            attn[i * tok_n : (i + 1) * tok_n, h * head_w : (h + 1) * head_w] = (
+                mixed / total
+            ).astype(bf16)
+
+    for e in range(m):
+        part[e] = jnp.dot(
+            attn[...], o_ref[:, e * width_q : (e + 1) * width_q], preferred_element_type=f32
+        ).astype(bf16)
+
+    def rs_copy(e):
+        peer = (mp + e) % m
+        return remote(part.at[peer], rs_buf.at[mp], rs_send.at[e], rs_recv.at[mp], (s, peer))
+
+    for e in range(1, m):
+        rs_copy(e).start()
+    summed = part[mp].astype(f32)
+    for e in range(1, m):
+        peer = (mp + e) % m
+        remote(
+            part.at[peer], rs_buf.at[peer], rs_send.at[e], rs_recv.at[peer], (s, peer)
+        ).wait_recv()
+        summed = summed + rs_buf[peer].astype(f32)
+    resid[s, mp] = (h_ref[...].astype(f32) + summed).astype(bf16)
+
+    def ag_copy(kind, bs, bm, device):
+        return remote(
+            resid.at[bs, bm], resid.at[bs, bm], ag_send.at[kind, bs, bm], ag_recv.at[bs, bm], device
+        )
+
+    def ag_wait(bs, bm):
+        ag_copy(0, bs, bm, dev_c).wait_recv()
+
+    def z_copy(dz):
+        return remote(
+            resid.at[s, mp],
+            resid.at[s, mp],
+            zg_send.at[dz],
+            ag_recv.at[s, mp],
+            (seq_of((z + dz) % nz, y), mp),
+        )
+
+    for dz in range(1, nz):
+        z_copy(dz).start()
+    for dz in range(nz):
+        bs, bm = seq_of((z + dz) % nz, y), mp
+        if dz:
+            ag_wait(bs, bm)
+        ag_copy(0, bs, bm, dev_a).start()
+        ag_copy(1, bs, bm, dev_b).start()
+        ag_copy(2, bs, bm, dev_c).start()
+    for dz in range(nz):
+        bs, bm = seq_of((z + dz) % nz, ya), mp_of(xa, c)
+        ag_wait(bs, bm)
+        ag_copy(1, bs, bm, dev_b).start()
+        ag_copy(2, bs, bm, dev_c).start()
+    for dz in range(nz):
+        for yy, xx in ((yb, xb), (1 - y, 1 - x)):
+            bs, bm = seq_of((z + dz) % nz, yy), mp_of(xx, c)
+            ag_wait(bs, bm)
+            ag_copy(2, bs, bm, dev_c).start()
+
+    for d in range(1, n):
+        peer = (s + d) % n
+        here = pl.ds(pl.multiple_of(peer * rows, rows), rows)
+        remote(
+            w_ref.at[:, peer], w_all.at[:, :, here], w_send.at[d], w_recv.at[peer], (peer, mp)
+        ).wait_recv()
+
+    def c_copy(t, xx):
+        return remote(
+            sums.at[t, mp_of(xx, 1 - c)],
+            c_buf.at[t, xx],
+            c_send.at[t, xx],
+            c_recv.at[t, xx],
+            dev_c,
+        )
+
+    def chunk(t, carry):
+        for xx in range(nx):
+            ag_wait(t, mp_of(xx, 1 - c))
+        total = jnp.zeros((tok, 1), f32)
+        for e in range(m):
+            piece = resid[t, e].astype(f32)
+            total = total + jnp.sum(piece * piece, axis=-1, keepdims=True)
+        factor = lax.rsqrt(total / (m * width_q) + norm_eps)
+        for e in range(m):
+            cols = slice(e * width_q, (e + 1) * width_q)
+            mlp_in[:, cols] = (resid[t, e].astype(f32) * factor * g_ref[:, cols]).astype(bf16)
+        dims = (((1,), (1,)), ((), ()))
+        gate = lax.dot_general(mlp_in[...], w_all[0], dims, preferred_element_type=f32)
+        up = lax.dot_general(mlp_in[...], w_all[1], dims, preferred_element_type=f32)
+        active = (gate / (1.0 + jnp.exp(-gate)) * up).astype(bf16)
+        for e in range(m):
+            sums[t, e] = jnp.dot(
+                active, w_all[2, :, e * width_q : (e + 1) * width_q], preferred_element_type=f32
+            ).astype(bf16)
+        for xx in range(nx):
+            c_copy(t, xx).start()
+        return carry
+
+    lax.fori_loop(0, n, chunk, 0)
+
+    def with_partner(bs, xx):
+        c_copy(bs, xx).wait_recv()
+        return sums[bs, mp_of(xx, c)].astype(f32) + c_buf[bs, xx].astype(f32)
+
+    def b_copy(kind, zz, yy, xx):
+        return remote(
+            sums.at[seq_of(zz, yy), mp_of(xx, c)],
+            b_buf.at[kind, zz],
+            b_send.at[kind, zz],
+            b_recv.at[kind, zz],
+            dev_b,
+        )
+
+    def a_copy(zz):
+        return remote(
+            sums.at[seq_of(zz, ya), mp_of(xa, c)],
+            a_buf.at[zz],
+            a_send.at[zz],
+            a_recv.at[zz],
+            dev_a,
+        )
+
+    def zs_copy(dz, slot):
+        zz = (z + dz) % nz
+        return remote(
+            sums.at[seq_of(zz, y), mp],
+            z_buf.at[slot],
+            zs_send.at[dz],
+            zs_recv.at[slot],
+            (seq_of(zz, y), mp),
+        )
+
+    order = list(range(1, nz)) + [0]
+    for kind, (yy, xx) in ((1, (1 - y, 1 - x)), (0, (yb, xb))):
+        for dz in order:
+            zz = (z + dz) % nz
+            bs = seq_of(zz, yy)
+            sums[bs, mp_of(xx, c)] = with_partner(bs, xx).astype(bf16)
+            b_copy(kind, zz, yy, xx).start()
+    for dz in order:
+        zz = (z + dz) % nz
+        bs = seq_of(zz, ya)
+        value = with_partner(bs, xa)
+        b_copy(1, zz, yb, xb).wait_recv()
+        sums[bs, mp_of(xa, c)] = (value + b_buf[1, zz].astype(f32)).astype(bf16)
+        a_copy(zz).start()
+    own = None
+    for dz in order:
+        zz = (z + dz) % nz
+        bs = seq_of(zz, y)
+        value = with_partner(bs, x)
+        b_copy(0, zz, yb, xb).wait_recv()
+        a_copy(zz).wait_recv()
+        value = value + b_buf[0, zz].astype(f32) + a_buf[zz].astype(f32)
+        if dz:
+            sums[bs, mp] = value.astype(bf16)
+            zs_copy(dz, z).start()
+        else:
+            own = value
+    for dz in range(1, nz):
+        slot = (z + dz) % nz
+        zs_copy(dz, slot).wait_recv()
+        own = own + z_buf[slot].astype(f32)
+    out_ref[...] = (resid[s, mp].astype(f32) + own).astype(bf16)
+
+    for d in range(1, n):
+        @pl.when((s + d) % n > s)
+        def _():
+            kv_copy(d).wait_send()
+
+        w_copy(d).wait_send()
+    for j in range(n):
+        @pl.when(j < s)
+        def _():
+            fw_copy(j, c).wait_send()
+    for e in range(1, m):
+        rs_copy(e).wait_send()
+    for dz in range(nz):
+        zz = (z + dz) % nz
+        if dz:
+            z_copy(dz).wait_send()
+            zs_copy(dz, z).wait_send()
+        ag_copy(0, seq_of(zz, y), mp, dev_a).wait_send()
+        ag_copy(1, seq_of(zz, y), mp, dev_b).wait_send()
+        ag_copy(1, seq_of(zz, ya), mp_of(xa, c), dev_b).wait_send()
+        for yy, xx in ((y, x), (ya, xa), (yb, xb), (1 - y, 1 - x)):
+            ag_copy(2, seq_of(zz, yy), mp_of(xx, c), dev_c).wait_send()
+        b_copy(0, zz, yb, xb).wait_send()
+        b_copy(1, zz, 1 - y, 1 - x).wait_send()
+        a_copy(zz).wait_send()
+    for t in range(n):
+        for xx in range(nx):
+            c_copy(t, xx).wait_send()
+
+
+def run_layer(n, m, queries, kv_here, weights, o_weight, own_in, gain):
+    tok, width_q = own_in.shape
+    seqs_n, heads_here, tok_n, head_w = queries.shape
+    width = m * width_q
+    _, _, ff_rows, rows = weights.shape
+    nz, nx = n // PAIR, m // PAIR
+    dt = jnp.bfloat16
+    dma = pltpu.SemaphoreType.DMA
+    block = (tok, width_q)
+    return pl.pallas_call(
+        functools.partial(layer_kernel, n, m),
+        out_shape=jax.ShapeDtypeStruct(block, dt),
+        in_specs=[pl.BlockSpec(memory_space=pltpu.VMEM)] * 6,
+        out_specs=pl.BlockSpec(memory_space=pltpu.VMEM),
+        scratch_shapes=[
+            pltpu.VMEM((2, n, seqs_n, tok_n, head_w), dt),
+            pltpu.VMEM((3, ff_rows, width), dt),
+            pltpu.VMEM((tok, heads_here * head_w), dt),
+            pltpu.VMEM((m,) + block, dt),
+            pltpu.VMEM((m,) + block, dt),
+            pltpu.VMEM((n, m) + block, dt),
+            pltpu.VMEM((tok, width), dt),
+            pltpu.VMEM((n, m) + block, dt),
+            pltpu.VMEM((n, nx) + block, dt),
+            pltpu.VMEM((2, nz) + block, dt),
+            pltpu.VMEM((nz,) + block, dt),
+            pltpu.VMEM((nz,) + block, dt),
+            dma((n,)),
+            dma((n,)),
+            dma((n,)),
+            dma((n,)),
+            dma((n,)),
+            dma((n,)),
+            dma((m,)),
+            dma((m,)),
+            dma((nz,)),
+            dma((3, n, m)),
+            dma((n, m)),
+            dma((n, nx)),
+            dma((n, nx)),
+            dma((2, nz)),
+            dma((2, nz)),
+            dma((nz,)),
+            dma((nz,)),
+            dma((nz,)),
+            dma((nz,)),
+        ],
+        compiler_params=pltpu.CompilerParams(
+            collective_id=0, has_side_effects=True, vmem_limit_bytes=VMEM_BYTES
+        ),
+    )(queries, kv_here, weights, o_weight, own_in, gain)
+
+
+def local_fast(
+    hidden_in,
+    attn_gain,
+    q_weight,
+    q_bias,
+    k_weight,
+    k_bias,
+    v_weight,
+    v_bias,
+    o_weight,
+    mlp_gain,
+    gate_weight,
+    up_weight,
+    down_weight,
+    lengths,
+):
+    seqs_n, tok_n, width = hidden_in.shape
+    n = lax.axis_size("seq")
+    m = lax.axis_size("mp")
+    seq_rank = lax.axis_index("seq")
+    mp_rank = lax.axis_index("mp")
+    heads_here = q_weight.shape[1] // HEAD
+    kv_index = mp_rank * heads_here // (HEADS // KV_HEADS)
+    quarter = width // m
+    flat_in = hidden_in.reshape(seqs_n * tok_n, width)
+    weights = jnp.stack([gate_weight.T, up_weight.T, down_weight.T])
+    weights = weights.reshape(3, n, gate_weight.shape[1] // n, gate_weight.shape[0])
+    normed = rms_scale(flat_in, attn_gain)
+    query_all = jnp.dot(normed, q_weight, preferred_element_type=jnp.float32) + q_bias
+    key_cols = lax.dynamic_slice_in_dim(k_weight, kv_index * HEAD, HEAD, 1)
+    value_cols = lax.dynamic_slice_in_dim(v_weight, kv_index * HEAD, HEAD, 1)
+    key_shift = lax.dynamic_slice_in_dim(k_bias, kv_index * HEAD, HEAD, 0)
+    value_shift = lax.dynamic_slice_in_dim(v_bias, kv_index * HEAD, HEAD, 0)
+    key_all = jnp.dot(normed, key_cols, preferred_element_type=jnp.float32) + key_shift
+    value_rows = (
+        jnp.dot(normed, value_cols, preferred_element_type=jnp.float32) + value_shift
+    ).astype(jnp.bfloat16)
+    positions = seq_rank * tok_n + jnp.arange(tok_n, dtype=jnp.int32)
+    rotated_q = rotate(
+        query_all.reshape(seqs_n, tok_n, heads_here, HEAD).transpose(0, 2, 1, 3), positions
+    ).astype(jnp.bfloat16)
+    rotated_k = rotate(key_all.reshape(seqs_n, tok_n, HEAD), positions).astype(jnp.bfloat16)
+    value_rows = value_rows.reshape(seqs_n, tok_n, HEAD)
+    own_in = lax.dynamic_slice_in_dim(flat_in, mp_rank * quarter, quarter, 1)
+    layer_part = run_layer(
+        n,
+        m,
+        rotated_q,
+        jnp.stack([rotated_k, value_rows]),
+        weights,
+        o_weight,
+        own_in,
+        mlp_gain[None, :],
+    )
+    in_share = own_in.astype(jnp.float32)
+    out_share = layer_part.astype(jnp.float32)
+    cross_part = jnp.sum(in_share * out_share, axis=-1).reshape(seqs_n, tok_n)
+    out_part = jnp.sum(out_share * out_share, axis=-1).reshape(seqs_n, tok_n)
+    cross, out_norm = lax.psum((cross_part, out_part), "mp")
+    in_wide = flat_in.astype(jnp.float32)
+    in_norm = jnp.sum(in_wide * in_wide, axis=-1).reshape(seqs_n, tok_n)
+    cosine = cross / jnp.sqrt((in_norm + norm_eps) * (out_norm + norm_eps))
+    valid = positions[None, :] < lengths[:, None]
+    influence = jnp.where(valid, 1.0 - cosine, 0.0)
+    seq_total = lax.psum(jnp.sum(influence, axis=1), "seq")
+    score = seq_total / lengths.astype(jnp.float32)
+    return (layer_part.reshape(seqs_n, tok_n, quarter), influence, score)
+
+
+def fits_on_chip(n, m, hidden_in, q_weight, gate_weight):
+    seqs_n, tok_n, width = hidden_in.shape
+    heads_here = q_weight.shape[1] // HEAD
+    ff_here, rows = gate_weight.shape[1], gate_weight.shape[0]
+    shared_kv = (HEADS // KV_HEADS) % (PAIR * heads_here) == 0
+    even = n % PAIR == 0 and m == PAIR * PAIR and ff_here % (16 * n) == 0
+    tiled = rows % 128 == 0 and tok_n % 16 == 0 and (n * tok_n) % 128 == 0
+    tiled = tiled and width % (128 * m) == 0
+    held = n * seqs_n * tok_n * width * 2 * 3
+    return shared_kv and even and tiled and held < VMEM_BYTES // 2
+
+
+def body(*args):
+    n, m = lax.axis_size("seq"), lax.axis_size("mp")
+    if fits_on_chip(n, m, args[0], args[2], args[10]):
+        return local_fast(*args)
+    return local(*args)
+
+
 def solution(mesh):
     placed = (
         P(None, "seq", None),
@@ -185,7 +673,7 @@
         P(),
     )
     return jax.shard_map(
-        local,
+        body,
         mesh=mesh,
         in_specs=placed,
         out_specs=(P(None, "seq", "mp"), P(None, "seq"), P()),

time: 448 us -> 225 us (0.50)
  waiting for transfers between devices: 295 us -> 0 us
  Pallas kernels: 0 us -> 167 us
  blocking collectives: 95.7 us -> 27.7 us
  matrix products: 22.6 us -> 4.45 us
  between operations: 15.9 us -> 0.81 us
  local copies, waits for them, and re-layouts: 2.51 us -> 10.8 us
    all_gather x3 -> x0, waiting for transfers between devices: 234 us -> none  [the longest x1 92.4 us: local(): lax.all_gather(down_weight, 'seq', axis=0, tiled=True)]
    pallas_call x0 -> x1, Pallas kernels: none -> 167 us  [run_layer(): pl.pallas_call(functools.partial(layer_kernel, n, m), out_shape=jax.Shape...]
    all_gather x2 -> x0, blocking collectives: 68.5 us -> none  [the longest x1 35.3 us: local(): key_piece = lax.all_gather(rotated_k, 'seq', axis=1, tiled=True)]
    psum x1 -> x0, waiting for transfers between devices: 35.9 us -> none  [local(): summed = lax.psum(projected.astype(jnp.bfloat16), 'mp').astype(jnp.float32)]
    reduce_scatter x1 -> x0, waiting for transfers between devices: 23.1 us -> none  [local(): lax.psum_scatter(down_part.astype(jnp.bfloat16), 'mp', scatter_dimension=...]
    dot_general x8 -> x3, matrix products: 22.6 us -> 4.45 us  [the longest x1 1.52 us: local_fast(): jnp.dot(normed, q_weight, preferred_element_type=jnp.float32) + q_bias]
  transfers between devices with their start and end apart: 5 -> 0, of which waited for: 5 -> 0; matrix products, arithmetic and copies ran while one was open for 2% -> 0% of each run, Pallas kernels for 0% -> 0%
where the time goes in v1:
time: 225 us; the launch traced here: 224 us
  Pallas kernels  167 us (74%)
  blocking collectives  27.7 us (12%)
  other arithmetic  13.5 us (6%)
  local copies, waits for them, and re-layouts  10.8 us (5%)
  matrix products  4.45 us (2%)
    pallas_call x1, Pallas kernels, run_layer(): pl.pallas_call(functools.partial(layer_kernel, n, m), out_shape=jax.Shape...  167 us
    psum x1, blocking collectives, local_fast(): seq_total = lax.psum(jnp.sum(influence, axis=1), 'seq')  20 us
    psum x1, blocking collectives, local_fast(): cross, out_norm = lax.psum((cross_part, out_part), 'mp')  7.74 us
    transpose x3, local copies, waits for them, and re-layouts, local_fast(): weights = jnp.stack([gate_weight.T, up_weight.T, down_weight.T])  4.56 us

profile of v1, /device:TPU:0, one launch (start us, length us, event | category | flops | bytes accessed | tf_op | source)
XLA Modules:
  0.0 224.1 jit_solution(15325677276298618683)
XLA Ops:
  0.7 1.7 multiply_reduce_fusion
  2.3 1.6 multiply_convert_fusion
  3.9 1.5 convolution_add_fusion
  5.4 2.0 reshape.225
  7.4 1.1 copy.27
  8.5 1.2 slice_negate_fusion
  9.8 0.3 fusion.11
  10.1 0.6 copy-done.4
  10.7 2.3 %fusion.4.q_ref = bf16[2,4,128,128]{3,2,1,0:T(8,128)(2,1)} fusion(f32[2,4,128,64]{3,2,1,0:T(8,128)} %get-tuple-element.10, f32[2,4,128,64]{3,2,1,0:T(8,128)} %get-tuple-element.9, f32[128,128]{1,0:T(8,128)S(1)} %get-tuple-element.14, f32[128,128]{1,0:T(8,128)S(1)} %get-tuple-element.13, f32[2,128,4,128]{3,2,1,0:T(4,128)} %reshape.225), kind=kLoop, calls=%fused_computation.14 | loop fusion | flops 655360 | bytes 1441792 | tf_op jit(solution)/shard_map/convert_element_type | solution.py:610
  13.1 1.5 fusion
  14.7 1.5 convolution_add_fusion.2
  16.4 0.7 pad_maximum_fusion.1.kv_ref
  17.1 2.3 %copy.23 = bf16[1408,256]{1,0:T(8,128)(2,1)} copy(bf16[1408,256]{0,1:T(8,128)(2,1)} %bitcast.39) | data formatting | bytes 1441792 | tf_op jit(solution)/shard_map/transpose | solution.py:595
  19.3 1.1 copy.22
  20.5 1.1 copy.21
  21.6 3.2 %pad_maximum_fusion.w_ref = bf16[3,8,176,256]{3,2,1,0:T(8,128)(2,1)} fusion(bf16[1,8,176,256]{3,2,1,0:T(8,128)(2,1)} %bitcast.33, bf16[1,8,176,256]{3,2,1,0:T(8,128)(2,1)} %bitcast.34, bf16[1,8,176,256]{3,2,1,0:T(8,128)(2,1)} %bitcast.35), kind=kLoop, calls=%fused_computation | loop fusion | flops 2162688 | bytes 4325376 | tf_op jit(solution)/shard_map/stack | solution.py:595
  24.8 0.7 constant_dynamic-slice_fusion.h_ref
  25.6 166.8 %shard_map.157 = bf16[256,512]{1,0:T(8,128)(2,1)} custom-call(bf16[2,4,128,128]{3,2,1,0:T(8,128)(2,1)} %fusion.4.q_ref, bf16[2,2,128,128]{3,2,1,0:T(8,128)(2,1)} %pad_maximum_fusion.1.kv_ref, bf16[3,8,176,256]{3,2,1,0:T(8,128)(2,1)} %pad_maximum_fusion.w_ref, bf16[512,2048]{1,0:T(8,128)(2,1)} %o_ref.1, bf16[256,512]{1,0:T(8,128)(2,1)} %constant_dynamic-slice_fusion.h_ref, ...), custom_call_target="tpu_custom_call" | custom-call | tf_op jit(solution)/shard_map/pallas_call | solution.py:526
  192.3 1.1 fusion.2
  193.5 7.7 %all-reduce = (f32[2,128]{1,0:T(2,128)S(1)}, f32[2,128]{1,0:T(2,128)S(1)}) all-reduce(f32[2,128]{1,0:T(2,128)S(1)} %bitcast.45, f32[2,128]{1,0:T(2,128)S(1)} %bitcast.44), channel_id=1, replica_groups=mesh['seq'=8,'mp'=4] {'mp'}, use_global_device_ids=true, to_apply=%region_2.3 | all-reduce | flops 512 | bytes 4096 | tf_op jit(solution)/shard_map/psum | solution.py:628
  201.2 0.7 fusion.15
  202.0 20.0 %psum.23 = f32[2]{0:T(128)S(1)} all-reduce(f32[2]{0:T(128)S(1)} %get-tuple-element.7), channel_id=1, replica_groups=mesh['seq'=8,'mp'=4] {'seq'}, use_global_device_ids=true, to_apply=%region_6.7 | all-reduce | flops 2 | bytes 16 | tf_op jit(solution)/shard_map/psum | solution.py:634
  221.9 0.5 convert_divide_fusion
  222.5 1.7 copy.29
  (32 shorter events, 0.5 us)
Async XLA Ops:
  0.6 3.3 %copy-start = (bf16[2048,512]{1,0:T(8,128)(2,1)S(1)}, bf16[2048,512]{1,0:T(8,128)(2,1)}, u32[]{:S(2)}) copy-start(bf16[2048,512]{1,0:T(8,128)(2,1)} %param.16) | copy-start | bytes 6291460
  0.6 3.2 %copy-start.9 = (f32[512]{0:T(512)S(1)}, f32[512]{0:T(512)}, u32[]{:S(2)}) copy-start(f32[512]{0:T(512)} %param.17) | copy-start | bytes 6148
  8.5 4.5 %copy-start.10 = (f32[256]{0:T(256)S(1)}, f32[256]{0:T(256)}, u32[]{:S(2)}) copy-start(f32[256]{0:T(256)} %param.21) | copy-start | bytes 3076
  9.7 4.9 %copy-start.11 = (f32[256]{0:T(256)S(1)}, f32[256]{0:T(256)}, u32[]{:S(2)}) copy-start(f32[256]{0:T(256)} %param.19) | copy-start | bytes 3076
  10.1 0.6 copy-start.4
  10.1 0.6 copy-start.6
  13.0 3.2 %copy-start.5 = (f32[128,128]{1,0:T(8,128)S(1)}, f32[128,128]{1,0:T(8,128)}, u32[]{:S(2)}) copy-start(f32[128,128]{1,0:T(8,128)} %copy-done.4) | copy-start | bytes 196612
  13.0 3.2 %copy-start.7 = (f32[128,128]{1,0:T(8,128)S(1)}, f32[128,128]{1,0:T(8,128)}, u32[]{:S(2)}) copy-start(f32[128,128]{1,0:T(8,128)} %copy-done.6) | copy-start | bytes 196612
  16.1 3.2 %copy-start.2 = (bf16[256,1408]{1,0:T(8,128)(2,1)S(1)}, bf16[256,1408]{1,0:T(8,128)(2,1)}, u32[]{:S(2)}) copy-start(bf16[256,1408]{1,0:T(8,128)(2,1)} %param.25) | copy-start | bytes 2162692
  16.1 4.3 %copy-start.3 = (bf16[256,1408]{1,0:T(8,128)(2,1)S(1)}, bf16[256,1408]{1,0:T(8,128)(2,1)}, u32[]{:S(2)}) copy-start(bf16[256,1408]{1,0:T(8,128)(2,1)} %param.24) | copy-start | bytes 2162692
  21.6 3.2 %copy-start.1 = (bf16[2,128,2048]{2,1,0:T(8,128)(2,1)S(1)}, bf16[2,128,2048]{2,1,0:T(8,128)(2,1)}, u32[]{:S(2)}) copy-start(bf16[2,128,2048]{2,1,0:T(8,128)(2,1)} %param.14) | copy-start | bytes 3145732
  25.6 175.7 %copy-start.8 = (s32[2]{0:T(128)S(1)}, s32[2]{0:T(128)}, u32[]{:S(2)}) copy-start(s32[2]{0:T(128)} %param.27) | copy-start | bytes 28

commit v2 on v1

--- a/solution.py
+++ b/solution.py
@@ -179,13 +179,26 @@
 def layer_kernel(
     n,
     m,
-    q_ref,
-    kv_ref,
+    x_ref,
+    ag_ref,
+    qw_ref,
+    qb_ref,
+    kw_ref,
+    kb_ref,
+    vw_ref,
+    vb_ref,
+    cos_ref,
+    sin_ref,
     w_ref,
     o_ref,
-    h_ref,
     g_ref,
+    len_ref,
     out_ref,
+    inf_ref,
+    tot_ref,
+    q_all,
+    stat,
+    tot_all,
     kv_all,
     w_all,
     attn,
@@ -217,6 +230,10 @@
     a_recv,
     zs_send,
     zs_recv,
+    st_send,
+    st_recv,
+    tt_send,
+    tt_recv,
 ):
     f32, bf16 = jnp.float32, jnp.bfloat16
     s = lax.axis_index("seq")
@@ -225,8 +242,14 @@
     nx = m // PAIR
     z, y = s // PAIR, s % PAIR
     x, c = mp // PAIR, mp % PAIR
-    tok, width_q = h_ref.shape
-    seqs_n, heads_here, tok_n, head_w = q_ref.shape
+    tok, width = x_ref.shape
+    width_q = width // m
+    tok_n, head_w = cos_ref.shape
+    seqs_n = tok // tok_n
+    heads_here = qw_ref.shape[1] // head_w
+    quarter = pl.ds(pl.multiple_of(mp * width_q, width_q), width_q)
+    kv_at = mp * heads_here // (HEADS // KV_HEADS)
+    kv_cols = pl.ds(pl.multiple_of(kv_at * head_w, head_w), head_w)
     rows = w_ref.shape[3]
 
     def seq_of(zz, yy):
@@ -260,7 +283,7 @@
 
     def kv_copy(d):
         return remote(
-            kv_ref.at[c], kv_all.at[c, s], kv_send.at[d], kv_recv.at[s], ((s + d) % n, mp)
+            kv_all.at[c, s], kv_all.at[c, s], kv_send.at[d], kv_recv.at[s], ((s + d) % n, mp)
         )
 
     def w_copy(d):
@@ -269,6 +292,22 @@
         return remote(
             w_ref.at[:, peer], w_all.at[:, :, here], w_send.at[d], w_recv.at[s], (peer, mp)
         )
+
+    wide = x_ref[...].astype(f32)
+    factor = lax.rsqrt(jnp.mean(wide * wide, axis=-1, keepdims=True) + norm_eps)
+    mlp_in[...] = (wide * factor * ag_ref[...]).astype(bf16)
+
+    def turn(values):
+        return values * cos_ref[...] + pltpu.roll(values, head_w // 2, 1) * sin_ref[...]
+
+    keys = jnp.dot(mlp_in[...], kw_ref[:, kv_cols], preferred_element_type=f32)
+    keys = keys + kb_ref[:, kv_cols]
+    vals = jnp.dot(mlp_in[...], vw_ref[:, kv_cols], preferred_element_type=f32)
+    vals = vals + vb_ref[:, kv_cols]
+    for i in range(seqs_n):
+        span = slice(i * tok_n, (i + 1) * tok_n)
+        kv_all[0, s, i] = turn(keys[span]).astype(bf16)
+        kv_all[1, s, i] = vals[span].astype(bf16)
 
     for d in range(1, n):
         @pl.when((s + d) % n > s)
@@ -278,14 +317,19 @@
     for d in range(1, n):
         w_copy(d).start()
 
-    kv_all[0, s] = kv_ref[0]
-    kv_all[1, s] = kv_ref[1]
+    for h in range(heads_here):
+        cols = slice(h * head_w, (h + 1) * head_w)
+        query = jnp.dot(mlp_in[...], qw_ref[:, cols], preferred_element_type=f32)
+        query = query + qb_ref[:, cols]
+        for i in range(seqs_n):
+            q_all[i, h] = turn(query[i * tok_n : (i + 1) * tok_n]).astype(bf16)
+
     w_all[:, :, pl.ds(pl.multiple_of(s * rows, rows), rows)] = w_ref[:, s]
     for j in range(n):
         @pl.when(j > s)
         def _():
-            kv_all[0, j] = jnp.zeros_like(kv_ref[0])
-            kv_all[1, j] = jnp.zeros_like(kv_ref[1])
+            kv_all[0, j] = jnp.zeros(kv_all.shape[2:], bf16)
+            kv_all[1, j] = jnp.zeros(kv_all.shape[2:], bf16)
 
     def fw_copy(j, cc):
         return remote(kv_all.at[cc, j], kv_all.at[cc, j], fw_send.at[j], fw_recv.at[j], dev_c)
@@ -293,7 +337,9 @@
     for j in range(n):
         @pl.when(j < s)
         def _():
-            remote(kv_ref.at[c], kv_all.at[c, j], kv_send.at[0], kv_recv.at[j], dev_c).wait_recv()
+            remote(
+                kv_all.at[c, s], kv_all.at[c, j], kv_send.at[0], kv_recv.at[j], dev_c
+            ).wait_recv()
             fw_copy(j, c).start()
 
     for j in range(n):
@@ -310,7 +356,7 @@
         vals = kv_all[1, :, i].reshape(n * tok_n, head_w)
         for h in range(heads_here):
             scores = lax.dot_general(
-                q_ref[i, h], keys, (((1,), (1,)), ((), ())), preferred_element_type=f32
+                q_all[i, h], keys, (((1,), (1,)), ((), ())), preferred_element_type=f32
             )
             scores = jnp.where(allowed, scores * scale, masked_score)
             top = jnp.max(scores, axis=-1, keepdims=True)
@@ -339,7 +385,7 @@
             part.at[peer], rs_buf.at[peer], rs_send.at[e], rs_recv.at[peer], (s, peer)
         ).wait_recv()
         summed = summed + rs_buf[peer].astype(f32)
-    resid[s, mp] = (h_ref[...].astype(f32) + summed).astype(bf16)
+    resid[s, mp] = (x_ref[:, quarter].astype(f32) + summed).astype(bf16)
 
     def ag_copy(kind, bs, bm, device):
         return remote(
@@ -482,7 +528,59 @@
         slot = (z + dz) % nz
         zs_copy(dz, slot).wait_recv()
         own = own + z_buf[slot].astype(f32)
-    out_ref[...] = (resid[s, mp].astype(f32) + own).astype(bf16)
+    layer_part = (resid[s, mp].astype(f32) + own).astype(bf16)
+    out_ref[...] = layer_part
+    share_out = layer_part.astype(f32)
+    share_in = x_ref[:, quarter].astype(f32)
+    lane = lax.broadcasted_iota(jnp.int32, (tok, 128), 1)
+    cross = jnp.sum(share_in * share_out, axis=-1, keepdims=True)
+    norm_out = jnp.sum(share_out * share_out, axis=-1, keepdims=True)
+    norm_in = jnp.sum(share_in * share_in, axis=-1, keepdims=True)
+    packed = jnp.where(lane == 0, cross, jnp.where(lane == 1, norm_out, norm_in))
+    stat[mp] = packed.T[:8]
+
+    def st_copy(e):
+        return remote(
+            stat.at[mp], stat.at[mp], st_send.at[e], st_recv.at[mp], (s, (mp + e) % m)
+        )
+
+    for e in range(1, m):
+        st_copy(e).start()
+    for e in range(1, m):
+        peer = (mp + e) % m
+        remote(stat.at[mp], stat.at[peer], st_send.at[e], st_recv.at[peer], (s, peer)).wait_recv()
+    full = stat[0]
+    for e in range(1, m):
+        full = full + stat[e]
+    cosine = full[0:1] / jnp.sqrt((full[2:3] + norm_eps) * (full[1:2] + norm_eps))
+    places = s * tok_n + lax.broadcasted_iota(jnp.int32, (1, tok_n), 1)
+    for i in range(seqs_n):
+        valid = places < len_ref[i : i + 1]
+        influence = jnp.where(valid, 1.0 - cosine[:, i * tok_n : (i + 1) * tok_n], 0.0)
+        inf_ref[i : i + 1] = influence
+        subtotal = jnp.sum(influence, axis=-1, keepdims=True)
+        tot_all[s, i : i + 1] = jnp.broadcast_to(subtotal, (1, 128))
+
+    def tt_copy(d):
+        return remote(
+            tot_all.at[s], tot_all.at[s], tt_send.at[d], tt_recv.at[s], ((s + d) % n, mp)
+        )
+
+    for d in range(1, n):
+        tt_copy(d).start()
+    for d in range(1, n):
+        peer = (s + d) % n
+        remote(
+            tot_all.at[s], tot_all.at[peer], tt_send.at[d], tt_recv.at[peer], (peer, mp)
+        ).wait_recv()
+    whole = tot_all[0]
+    for j in range(1, n):
+        whole = whole + tot_all[j]
+    tot_ref[...] = whole
+    for e in range(1, m):
+        st_copy(e).wait_send()
+    for d in range(1, n):
+        tt_copy(d).wait_send()
 
     for d in range(1, n):
         @pl.when((s + d) % n > s)
@@ -514,21 +612,29 @@
             c_copy(t, xx).wait_send()
 
 
-def run_layer(n, m, queries, kv_here, weights, o_weight, own_in, gain):
-    tok, width_q = own_in.shape
-    seqs_n, heads_here, tok_n, head_w = queries.shape
-    width = m * width_q
-    _, _, ff_rows, rows = weights.shape
+def run_layer(n, m, seqs_n, *operands):
+    tok, width = operands[0].shape
+    tok_n, head_w = operands[8].shape
+    heads_here = operands[2].shape[1] // head_w
+    ff_rows = operands[10].shape[2]
     nz, nx = n // PAIR, m // PAIR
     dt = jnp.bfloat16
     dma = pltpu.SemaphoreType.DMA
-    block = (tok, width_q)
+    block = (tok, width // m)
+    vmem = pl.BlockSpec(memory_space=pltpu.VMEM)
     return pl.pallas_call(
         functools.partial(layer_kernel, n, m),
-        out_shape=jax.ShapeDtypeStruct(block, dt),
-        in_specs=[pl.BlockSpec(memory_space=pltpu.VMEM)] * 6,
-        out_specs=pl.BlockSpec(memory_space=pltpu.VMEM),
+        out_shape=(
+            jax.ShapeDtypeStruct(block, dt),
+            jax.ShapeDtypeStruct((seqs_n, tok_n), jnp.float32),
+            jax.ShapeDtypeStruct((seqs_n, 128), jnp.float32),
+        ),
+        in_specs=[vmem] * len(operands),
+        out_specs=(vmem, vmem, vmem),
         scratch_shapes=[
+            pltpu.VMEM((seqs_n, heads_here, tok_n, head_w), dt),
+            pltpu.VMEM((m, 8, tok), jnp.float32),
+            pltpu.VMEM((n, seqs_n, 128), jnp.float32),
             pltpu.VMEM((2, n, seqs_n, tok_n, head_w), dt),
             pltpu.VMEM((3, ff_rows, width), dt),
             pltpu.VMEM((tok, heads_here * head_w), dt),
@@ -560,11 +666,15 @@
             dma((nz,)),
             dma((nz,)),
             dma((nz,)),
+            dma((m,)),
+            dma((m,)),
+            dma((n,)),
+            dma((n,)),
         ],
         compiler_params=pltpu.CompilerParams(
             collective_id=0, has_side_effects=True, vmem_limit_bytes=VMEM_BYTES
         ),
-    )(queries, kv_here, weights, o_weight, own_in, gain)
+    )(*operands)
 
 
 def local_fast(
@@ -587,53 +697,36 @@
     n = lax.axis_size("seq")
     m = lax.axis_size("mp")
     seq_rank = lax.axis_index("seq")
-    mp_rank = lax.axis_index("mp")
-    heads_here = q_weight.shape[1] // HEAD
-    kv_index = mp_rank * heads_here // (HEADS // KV_HEADS)
-    quarter = width // m
     flat_in = hidden_in.reshape(seqs_n * tok_n, width)
     weights = jnp.stack([gate_weight.T, up_weight.T, down_weight.T])
     weights = weights.reshape(3, n, gate_weight.shape[1] // n, gate_weight.shape[0])
-    normed = rms_scale(flat_in, attn_gain)
-    query_all = jnp.dot(normed, q_weight, preferred_element_type=jnp.float32) + q_bias
-    key_cols = lax.dynamic_slice_in_dim(k_weight, kv_index * HEAD, HEAD, 1)
-    value_cols = lax.dynamic_slice_in_dim(v_weight, kv_index * HEAD, HEAD, 1)
-    key_shift = lax.dynamic_slice_in_dim(k_bias, kv_index * HEAD, HEAD, 0)
-    value_shift = lax.dynamic_slice_in_dim(v_bias, kv_index * HEAD, HEAD, 0)
-    key_all = jnp.dot(normed, key_cols, preferred_element_type=jnp.float32) + key_shift
-    value_rows = (
-        jnp.dot(normed, value_cols, preferred_element_type=jnp.float32) + value_shift
-    ).astype(jnp.bfloat16)
+    half = HEAD // 2
+    inv_freq = rope_base ** (-(jnp.arange(half, dtype=jnp.float32) * 2.0) / HEAD)
     positions = seq_rank * tok_n + jnp.arange(tok_n, dtype=jnp.int32)
-    rotated_q = rotate(
-        query_all.reshape(seqs_n, tok_n, heads_here, HEAD).transpose(0, 2, 1, 3), positions
-    ).astype(jnp.bfloat16)
-    rotated_k = rotate(key_all.reshape(seqs_n, tok_n, HEAD), positions).astype(jnp.bfloat16)
-    value_rows = value_rows.reshape(seqs_n, tok_n, HEAD)
-    own_in = lax.dynamic_slice_in_dim(flat_in, mp_rank * quarter, quarter, 1)
-    layer_part = run_layer(
+    angles = positions.astype(jnp.float32)[:, None] * inv_freq[None, :]
+    sines = jnp.sin(angles)
+    cosines = jnp.cos(angles)
+    layer_part, influence, totals = run_layer(
         n,
         m,
-        rotated_q,
-        jnp.stack([rotated_k, value_rows]),
+        seqs_n,
+        flat_in,
+        attn_gain[None, :],
+        q_weight,
+        q_bias[None, :],
+        k_weight,
+        k_bias[None, :],
+        v_weight,
+        v_bias[None, :],
+        jnp.concatenate([cosines, cosines], axis=-1),
+        jnp.concatenate([-sines, sines], axis=-1),
         weights,
         o_weight,
-        own_in,
         mlp_gain[None, :],
-    )
-    in_share = own_in.astype(jnp.float32)
-    out_share = layer_part.astype(jnp.float32)
-    cross_part = jnp.sum(in_share * out_share, axis=-1).reshape(seqs_n, tok_n)
-    out_part = jnp.sum(out_share * out_share, axis=-1).reshape(seqs_n, tok_n)
-    cross, out_norm = lax.psum((cross_part, out_part), "mp")
-    in_wide = flat_in.astype(jnp.float32)
-    in_norm = jnp.sum(in_wide * in_wide, axis=-1).reshape(seqs_n, tok_n)
-    cosine = cross / jnp.sqrt((in_norm + norm_eps) * (out_norm + norm_eps))
-    valid = positions[None, :] < lengths[:, None]
-    influence = jnp.where(valid, 1.0 - cosine, 0.0)
-    seq_total = lax.psum(jnp.sum(influence, axis=1), "seq")
-    score = seq_total / lengths.astype(jnp.float32)
-    return (layer_part.reshape(seqs_n, tok_n, quarter), influence, score)
+        jnp.broadcast_to(lengths[:, None], (seqs_n, tok_n)),
+    )
+    score = totals[:, 0] / lengths.astype(jnp.float32)
+    return (layer_part.reshape(seqs_n, tok_n, width // m), influence, score)
 
 
 def fits_on_chip(n, m, hidden_in, q_weight, gate_weight):
@@ -642,7 +735,7 @@
     ff_here, rows = gate_weight.shape[1], gate_weight.shape[0]
     shared_kv = (HEADS // KV_HEADS) % (PAIR * heads_here) == 0
     even = n % PAIR == 0 and m == PAIR * PAIR and ff_here % (16 * n) == 0
-    tiled = rows % 128 == 0 and tok_n % 16 == 0 and (n * tok_n) % 128 == 0
+    tiled = rows % 128 == 0 and tok_n % 128 == 0
     tiled = tiled and width % (128 * m) == 0
     held = n * seqs_n * tok_n * width * 2 * 3
     return shared_kv and even and tiled and held < VMEM_BYTES // 2

time: 225 us -> 194 us (0.86)
  blocking collectives: 27.7 us -> 0 us
  Pallas kernels: 167 us -> 184 us
  other arithmetic: 13.5 us -> 3.2 us
  local copies, waits for them, and re-layouts: 10.8 us -> 6.23 us
  matrix products: 4.45 us -> 0 us
    psum x2 -> x0, blocking collectives: 27.7 us -> none  [the longest x1 20 us: local_fast(): seq_total = lax.psum(jnp.sum(influence, axis=1), 'seq')]
    pallas_call x1, Pallas kernels: 167 us -> 184 us  [run_layer(): pl.pallas_call(functools.partial(layer_kernel, n, m), out_shape=(jax.Shap...]
    dot_general x3 -> x0, matrix products: 4.45 us -> none  [the longest x1 1.52 us: local_fast(): jnp.dot(normed, q_weight, preferred_element_type=jnp.float32) + q_bias]
    convert_element_type x4 -> x1, other arithmetic: 3.93 us -> 0.01 us  [local_fast(): angles = positions.astype(jnp.float32)[:, None] * inv_freq[None, :]]
    reduce_sum x3 -> x0, other arithmetic: 3.53 us -> none  [the longest x1 1.66 us: rms_scale(): jnp.mean(widened * widened, axis=-1, keepdims=True) + norm_eps]
    reshape x2 -> x0, local copies, waits for them, and re-layouts: 3.07 us -> none  [local_fast(): query_all.reshape(seqs_n, tok_n, heads_here, HEAD).transpose(0, 2, 1, 3)]
    transpose x3, local copies, waits for them, and re-layouts: 4.56 us -> 1.94 us  [local_fast(): weights = jnp.stack([gate_weight.T, up_weight.T, down_weight.T])]
where the time goes in v2:
time: 194 us
  Pallas kernels  184 us (95%)
  local copies, waits for them, and re-layouts  6.23 us (3%)
  other arithmetic  3.2 us (2%)
    pallas_call x1, Pallas kernels, run_layer(): pl.pallas_call(functools.partial(layer_kernel, n, m), out_shape=(jax.Shap...  184 us

profile of v2, /device:TPU:0, one launch (start us, length us, event | category | flops | bytes accessed | tf_op | source)
XLA Modules:
  0.0 193.9 jit_solution(4040124703405071531)
XLA Ops:
  0.6 0.0 copy-start
  0.6 0.0 copy-start.1
  0.7 0.3 fusion
  1.0 0.7 pad_maximum_fusion.1
  1.7 1.4 copy.22
  3.1 0.0 copy-done
  3.1 0.3 copy.20
  3.4 0.0 copy-done.1
  3.4 0.3 copy.21
  3.7 0.0 copy-start.2
  3.7 1.6 pad_maximum_fusion.w_ref
  5.3 0.0 copy-done.2
  5.3 0.6 broadcast_in_dim.28.len_ref
  6.0 183.7 %shard_map.157 = (bf16[256,512]{1,0:T(8,128)(2,1)}, f32[2,128]{1,0:T(2,128)}, f32[2,128]{1,0:T(2,128)}) custom-call(bf16[256,2048]{1,0:T(8,128)(2,1)} %bitcast.16, f32[1,2048]{1,0:T(1,128)} %bitcast.21, bf16[2048,512]{1,0:T(8,128)(2,1)} %qw_ref.1, f32[1,512]{1,0:T(1,128)} %bitcast.23, bf16[2048,256]{1,0:T(8,128)(2,1)} %kw_ref.1, f32[1,256]{1,0:T(1,128)} %bitcast.24, ...), custom_call_target="tpu_custom_call" | custom-call | tf_op jit(solution)/shard_map/pallas_call | solution.py:625
  189.7 0.8 slice_reduce_fusion
  190.5 0.5 convert_divide_fusion
  191.0 1.7 copy.25
  192.7 1.2 copy.26
  (2 shorter events, 0.0 us)
Async XLA Ops:
  0.6 2.5 %copy-start = (bf16[256,1408]{1,0:T(8,128)(2,1)S(1)}, bf16[256,1408]{1,0:T(8,128)(2,1)}, u32[]{:S(2)}) copy-start(bf16[256,1408]{1,0:T(8,128)(2,1)} %param.24) | copy-start | bytes 2162692
  0.6 2.8 %copy-start.1 = (bf16[256,1408]{1,0:T(8,128)(2,1)S(1)}, bf16[256,1408]{1,0:T(8,128)(2,1)}, u32[]{:S(2)}) copy-start(bf16[256,1408]{1,0:T(8,128)(2,1)} %param.25) | copy-start | bytes 2162692
  3.7 1.6 copy-start.2

commit v3 on v2

--- a/solution.py
+++ b/solution.py
@@ -418,11 +418,14 @@
         ag_wait(bs, bm)
         ag_copy(1, bs, bm, dev_b).start()
         ag_copy(2, bs, bm, dev_c).start()
-    for dz in range(nz):
-        for yy, xx in ((yb, xb), (1 - y, 1 - x)):
+
+    def pass_on(yy, xx):
+        for dz in range(nz):
             bs, bm = seq_of((z + dz) % nz, yy), mp_of(xx, c)
             ag_wait(bs, bm)
             ag_copy(2, bs, bm, dev_c).start()
+
+    pass_on(yb, xb)
 
     for d in range(1, n):
         peer = (s + d) % n
@@ -463,7 +466,15 @@
             c_copy(t, xx).start()
         return carry
 
-    lax.fori_loop(0, n, chunk, 0)
+    def chunks(yy):
+        def one(dz, carry):
+            return chunk(seq_of((z + dz) % nz, yy), carry)
+
+        lax.fori_loop(0, nz, one, 0)
+
+    chunks(y)
+    pass_on(1 - y, 1 - x)
+    chunks(1 - y)
 
     def with_partner(bs, xx):
         c_copy(bs, xx).wait_recv()

time: 194 us -> 188 us (0.969)
  Pallas kernels: 184 us -> 178 us
    pallas_call x1, Pallas kernels: 184 us -> 178 us  [run_layer(): pl.pallas_call(functools.partial(layer_kernel, n, m), out_shape=(jax.Shap...]
where the time goes in v3:
time: 188 us
  Pallas kernels  178 us (95%)
  local copies, waits for them, and re-layouts  6.23 us (3%)
  other arithmetic  3.2 us (2%)
    pallas_call x1, Pallas kernels, run_layer(): pl.pallas_call(functools.partial(layer_kernel, n, m), out_shape=(jax.Shap...  178 us

profile of v3, /device:TPU:0, one launch (start us, length us, event | category | flops | bytes accessed | tf_op | source)
XLA Modules:
  0.0 188.0 jit_solution(6955242341280438667)
XLA Ops:
  0.6 0.0 copy-start
  0.6 0.0 copy-start.1
  0.7 0.3 fusion
  1.0 0.7 pad_maximum_fusion.1
  1.7 1.4 copy.22
  3.1 0.0 copy-done
  3.1 0.3 copy.20
  3.4 0.0 copy-done.1
  3.4 0.3 copy.21
  3.7 0.0 copy-start.2
  3.7 1.6 pad_maximum_fusion.w_ref
  5.3 0.0 copy-done.2
  5.3 0.6 broadcast_in_dim.28.len_ref
  6.0 177.9 %shard_map.157 = (bf16[256,512]{1,0:T(8,128)(2,1)}, f32[2,128]{1,0:T(2,128)}, f32[2,128]{1,0:T(2,128)}) custom-call(bf16[256,2048]{1,0:T(8,128)(2,1)} %bitcast.16, f32[1,2048]{1,0:T(1,128)} %bitcast.21, bf16[2048,512]{1,0:T(8,128)(2,1)} %qw_ref.1, f32[1,512]{1,0:T(1,128)} %bitcast.23, bf16[2048,256]{1,0:T(8,128)(2,1)} %kw_ref.1, f32[1,256]{1,0:T(1,128)} %bitcast.24, ...), custom_call_target="tpu_custom_call" | custom-call | tf_op jit(solution)/shard_map/pallas_call | solution.py:636
  183.9 0.8 slice_reduce_fusion
  184.6 0.5 convert_divide_fusion
  185.2 1.7 copy.25
  186.8 1.2 copy.26
  (2 shorter events, 0.0 us)
Async XLA Ops:
  0.6 2.5 %copy-start = (bf16[256,1408]{1,0:T(8,128)(2,1)S(1)}, bf16[256,1408]{1,0:T(8,128)(2,1)}, u32[]{:S(2)}) copy-start(bf16[256,1408]{1,0:T(8,128)(2,1)} %param.24) | copy-start | bytes 2162692
  0.6 2.8 %copy-start.1 = (bf16[256,1408]{1,0:T(8,128)(2,1)S(1)}, bf16[256,1408]{1,0:T(8,128)(2,1)}, u32[]{:S(2)}) copy-start(bf16[256,1408]{1,0:T(8,128)(2,1)} %param.25) | copy-start | bytes 2162692
  3.7 1.6 copy-start.2
